TPU v7x, 32 devices: a whole 2x2x4 slice. The times are simulated.
32 devices in a mesh: expert: 4 (over y, x), ffn: 8 (over z, core).
Axes of the slice: x: 2, y: 2, z: 4, core: 2. Of those that a mesh axis runs over, the one named last changes fastest.
Arguments:
- tokens: bfloat16 [1024, 4096], P('expert'), may hold values from -6 to 6
- router_gates: float32 [1024, 2], P('expert'), may hold values from 0.1 to 1
- routes: int32 [1024, 2], P('expert'), may hold values from 0 to 3, all different within a row; in each aligned block of 256 rows (0 to 255, 256 to 511, ...) at most 256 rows name the same one
- gate_proj: bfloat16 [4, 4096, 14336], P('expert', None, 'ffn'), may hold values from -0.09375 to 0.09375
- up_proj: bfloat16 [4, 4096, 14336], P('expert', None, 'ffn'), may hold values from -0.09375 to 0.09375
- down_proj: bfloat16 [4, 14336, 4096], P('expert', 'ffn'), may hold values from -0.0625 to 0.0625
Outputs:
- mixed: bfloat16 [1024, 4096], P('expert', 'ffn')
Inputs may be any that keep to these rules, and one draw needn't show every extreme that they name: `routes`: the 2 experts of a token differ. Among the tokens of one index of the expert axis (aligned blocks of 256 tokens) no expert is chosen by more than 256 tokens, and in some blocks one expert is chosen by exactly 256.
All inputs are finite; a program needn't handle non-finite values.
Results may differ from a plain program's by a relative error of at most 0.017.
Values may be sent and summed in bfloat16 or wider, within the bound.
A program may use at most 128 MiB of HBM per device.

v0:
```python
import jax
import jax.numpy as jnp
from jax import lax
from jax.sharding import PartitionSpec as P

TOP = 2


def per_device(tokens, router_gates, routes, gate_proj, up_proj, down_proj):
    experts = lax.axis_size("expert")
    groups = lax.axis_size("ffn")
    tok_rows = tokens.shape[0]
    width_all = tokens.shape[1]
    capacity = 2 * TOP * tok_rows // experts
    slots_all = experts * capacity
    col_width = width_all // groups
    gate_matrix = gate_proj[0]
    up_matrix = up_proj[0]
    down_matrix = down_proj[0]
    flattened = routes.reshape(-1)
    chosen = (flattened[:, None] == jnp.arange(experts, dtype=jnp.int32)[None, :]).astype(jnp.int32)
    ranking = jnp.cumsum(chosen, axis=0) - chosen
    targets = (flattened * capacity + jnp.sum(ranking * chosen, axis=1)).reshape(tok_rows, TOP)
    slot_ids = jnp.arange(slots_all, dtype=jnp.int32)
    matches = targets[:, :, None] == slot_ids[None, None, :]
    placing = jnp.any(matches, axis=1).astype(jnp.bfloat16)
    weighting = jnp.sum(jnp.where(matches, router_gates[:, :, None], 0.0), axis=1)
    outgoing = lax.dot_general(
        placing, tokens, (((0,), (0,)), ((), ())), preferred_element_type=jnp.float32
    )
    outgoing = outgoing.astype(jnp.bfloat16).reshape(experts, capacity, width_all)
    arrived = lax.all_to_all(outgoing, "expert", split_axis=0, concat_axis=0, tiled=True).reshape(
        slots_all, width_all
    )
    gate_act = jnp.dot(arrived, gate_matrix, preferred_element_type=jnp.float32)
    up_act = jnp.dot(arrived, up_matrix, preferred_element_type=jnp.float32)
    hidden = (jax.nn.silu(gate_act) * up_act).astype(jnp.bfloat16)
    summed = lax.psum_scatter(
        lax.dot_general(
            down_matrix, hidden, (((0,), (1,)), ((), ())), preferred_element_type=jnp.float32
        ).astype(jnp.bfloat16),
        "ffn",
        scatter_dimension=0,
        tiled=True,
    ).astype(jnp.float32)
    returned_rows = lax.all_to_all(
        summed.reshape(col_width, experts, capacity).astype(jnp.bfloat16),
        "expert",
        split_axis=1,
        concat_axis=1,
        tiled=True,
    ).astype(jnp.float32)
    mixed = lax.dot_general(
        weighting,
        returned_rows.reshape(col_width, slots_all),
        (((1,), (1,)), ((), ())),
        precision=lax.Precision.HIGHEST,
        preferred_element_type=jnp.float32,
    )
    return mixed.astype(jnp.bfloat16)


def solution(mesh):
    in_specs = (
        P("expert", None),
        P("expert", None),
        P("expert", None),
        P("expert", None, "ffn"),
        P("expert", None, "ffn"),
        P("expert", "ffn", None),
    )
    out_specs = P("expert", "ffn")
    return jax.shard_map(
        per_device, mesh=mesh, in_specs=in_specs, out_specs=out_specs, check_vma=False
    )
```

profile of v0, /device:TPU:0, one launch (start us, length us, event | category | flops | bytes accessed | tf_op | source)
XLA Modules:
  0.0 286.3 jit_solution(17005412014355842881)
XLA Ops:
  6.5 0.0 copy-start
  6.5 0.0 reduce-scatter.2.cloned.1.call-start
  6.5 1.0 copy.19
  7.5 0.1 eq.42
  7.7 0.1 eq.38
  7.8 1.2 reduce-window.6
  9.0 0.2 slice_reduce_fusion
  9.2 0.2 reduce-window.9
  9.4 0.1 add_bitcast_fusion
  9.5 0.1 reduce_sum.21
  9.7 0.1 copy.21
  9.8 0.7 multiply_add_fusion
  10.5 0.3 fusion.10
  10.7 0.0 copy-done
  10.7 2.4 convolution_convert_fusion
  13.1 97.8 %all_to_all.10 = bf16[4,256,4096]{2,1,0:T(8,128)(2,1)S(1)} all-to-all(bf16[4,256,4096]{2,1,0:T(8,128)(2,1)S(1)} %bitcast.45), channel_id=1, replica_groups=mesh['expert'=4,'ffn'=8] {'expert'}, dimensions={0} | all-to-all | bytes 16777216 | tf_op jit(solution)/shard_map/all_to_all | solution.py:32
  110.9 18.7 %fusion.4 = f32[1024,1792]{1,0:T(8,128)S(1)} fusion(bf16[1024,4096]{1,0:T(8,128)(2,1)S(1)} %bitcast.46, bf16[1,4096,1792]{2,1,0:T(8,128)(2,1)} %param.9), kind=kOutput, calls=%fused_computation.4 | convolution fusion | flops 15032385536 | bytes 30408704 | tf_op jit(solution)/shard_map/dot_general | solution.py:35
  129.6 21.1 %multiply_convert_fusion = bf16[1024,1792]{1,0:T(8,128)(2,1)S(1)} fusion(f32[1024,1792]{1,0:T(8,128)S(1)} %fusion.4, bf16[1024,4096]{1,0:T(8,128)(2,1)S(1)} %bitcast.47, bf16[1,4096,1792]{2,1,0:T(8,128)(2,1)} %param.10), kind=kOutput, calls=%fused_computation.8 | convolution fusion | flops 15043395584 | bytes 34078720 | tf_op jit(solution)/shard_map/dot_general | solution.py:36
  150.7 0.0 copy-start.1
  150.7 20.9 %convert_bitcast_fusion = bf16[4096,1024]{0,1:T(8,128)(2,1)} fusion(bf16[1024,1792]{1,0:T(8,128)(2,1)S(1)} %multiply_convert_fusion, bf16[1,1792,4096]{2,1,0:T(8,128)(2,1)} %param.11), kind=kOutput, calls=%fused_computation.6 | convolution fusion | flops 15036579840 | bytes 26738688 | tf_op jit(solution)/shard_map/dot_general | solution.py:39
  171.5 0.0 copy-start.2
  171.5 0.0 reduce-scatter.2.cloned.1.call-update
  171.6 89.4 %reduce-scatter.2.cloned.1.call-done = bf16[512,1024]{0,1:T(8,128)(2,1)} async-done(((bf16[4096,1024]{0,1:T(8,128)(2,1)}), bf16[512,1024]{0,1:T(8,128)(2,1)}) %reduce-scatter.2.cloned.1.call-update) | async-done | bytes 1048592 | tf_op jit(solution)/shard_map/reduce_scatter | solution.py:38
  261.0 3.6 %all-to-all-start.1 = ((bf16[512,4,256]{0,2,1:T(8,128)(2,1)}), bf16[512,4,256]{0,2,1:T(8,128)(2,1)S(1)}, u32[]{:S(2)}, u32[]{:S(2)}) async-start(bf16[512,4,256]{0,2,1:T(8,128)(2,1)} %bitcast.49), calls=%async_computation.2 | async-start | bytes 2097152 | tf_op jit(solution)/shard_map/all_to_all | solution.py:46
  264.6 0.0 copy-done.2
  264.6 1.3 select_reduce_fusion
  265.9 10.6 %all-to-all-done.1 = bf16[512,4,256]{0,2,1:T(8,128)(2,1)S(1)} async-done(((bf16[512,4,256]{0,2,1:T(8,128)(2,1)}), bf16[512,4,256]{0,2,1:T(8,128)(2,1)S(1)}, u32[]{:S(2)}, u32[]{:S(2)}) %all-to-all-start.1) | async-done | bytes 1048608 | tf_op jit(solution)/shard_map/all_to_all | solution.py:46
  276.5 2.9 %convolution_convert_fusion.1 = bf16[256,512]{1,0:T(8,128)(2,1)} fusion(f32[256,1024]{1,0:T(8,128)} %select_reduce_fusion, bf16[512,1024]{0,1:T(8,128)(2,1)S(1)} %bitcast.48), kind=kOutput, calls=%fused_computation.12 | convolution fusion | flops 1610743808 | bytes 2359296 | tf_op jit(solution)/shard_map/dot_general | solution.py:53
  279.4 0.0 copy-done.1
  (2 shorter events, 0.0 us)
Async XLA Ops:
  6.5 4.2 %copy-start = (bf16[256,4096]{1,0:T(8,128)(2,1)S(1)}, bf16[256,4096]{1,0:T(8,128)(2,1)}, u32[]{:S(2)}) copy-start(bf16[256,4096]{1,0:T(8,128)(2,1)} %param.6) | copy-start | bytes 6291460
  6.5 254.4 %reduce-scatter.2.cloned.1.call-start = ((), (), s32[]{:S(2)}) async-start(), calls=%async_computation.3 | async-start | bytes 9437184 | tf_op jit(solution)/shard_map/reduce_scatter | solution.py:38
  150.7 128.8 %copy-start.1 = (bf16[256,4096]{1,0:T(8,128)(2,1)S(1)}, bf16[256,4096]{1,0:T(8,128)(2,1)}, u32[]{:S(2)}) copy-start(bf16[256,4096]{1,0:T(8,128)(2,1)} %param.6) | copy-start | bytes 6291460
  171.5 93.1 %copy-start.2 = (f32[256,2]{0,1:T(2,128)S(1)}, f32[256,2]{0,1:T(2,128)}, u32[]{:S(2)}) copy-start(f32[256,2]{0,1:T(2,128)} %param.7) | copy-start | bytes 6148
  261.0 15.5 %all-to-all-start.1 = ((bf16[512,4,256]{0,2,1:T(8,128)(2,1)}), bf16[512,4,256]{0,2,1:T(8,128)(2,1)S(1)}, u32[]{:S(2)}, u32[]{:S(2)}) async-start(bf16[512,4,256]{0,2,1:T(8,128)(2,1)} %bitcast.49), calls=%async_computation.2 | async-start | bytes 2097152 | tf_op jit(solution)/shard_map/all_to_all | solution.py:46
Sparse Core Ops, SparseCore 0:
  171.7 89.2 reduce-scatter.1
where the time goes:
time: 287 us; the launch traced here: 286 us
  waiting for transfers between devices  100 us (35%)
  blocking collectives  97.8 us (34%)
  matrix products  65.9 us (23%)
  between operations  13.5 us (5%)
  other arithmetic  3.72 us (1%)
  starting transfers between devices  3.65 us (1%)
    all_to_all x1, blocking collectives, per_device(): lax.all_to_all(outgoing, 'expert', split_axis=0, concat_axis=0, tiled=True)  97.8 us
    reduce_scatter x1, waiting for transfers between devices, per_device(): lax.psum_scatter(lax.dot_general(down_matrix, hidden, (((0,), (1,)), ((),...  89.4 us
    dot_general x1, matrix products, per_device(): up_act = jnp.dot(arrived, up_matrix, preferred_element_type=jnp.float32)  21.1 us
    dot_general x1, matrix products, per_device(): lax.dot_general(down_matrix, hidden, (((0,), (1,)), ((), ())), preferred_...  20.9 us
    dot_general x1, matrix products, per_device(): gate_act = jnp.dot(arrived, gate_matrix, preferred_element_type=jnp.float32)  18.7 us
    all_to_all x1, waiting for transfers between devices, per_device(): lax.all_to_all(summed.reshape(col_width, experts, capacity).astype(jnp.bf...  10.6 us
  transfers between devices with their start and end apart: 2, of which 2 were waited for; matrix products, arithmetic and copies ran while one was open for 0% of the time, Pallas kernels for 0%

commit v1 on v0

v1 whole, which is shorter than its diff:
```python
import functools

import jax
import jax.numpy as jnp
from jax import lax
from jax.experimental import pallas as pl
from jax.experimental.pallas import tpu as pltpu
from jax.sharding import PartitionSpec as P


def swap(value, axis, bit):
    size = lax.axis_size(axis)
    return lax.ppermute(value, axis, [(i, i ^ bit) for i in range(size)])


def after(value, *others):
    return lax.optimization_barrier((value,) + others)[0]


def expert_kernel(blocks, core_ref, x_ref, w_ref, gate_ref, up_ref, down_ref, keep_ref, give_ref, acc):
    step = pl.program_id(0)

    @pl.when(step == 0)
    def clear():
        acc[...] = jnp.zeros_like(acc)

    gate_act = jnp.dot(x_ref[...], gate_ref[...], preferred_element_type=jnp.float32)
    up_act = jnp.dot(x_ref[...], up_ref[...], preferred_element_type=jnp.float32)
    hidden = gate_act / (1.0 + jnp.exp(-gate_act)) * up_act * w_ref[...]
    acc[...] += jnp.dot(
        hidden.astype(jnp.bfloat16), down_ref[...], preferred_element_type=jnp.float32
    )

    @pl.when(step == pl.num_programs(0) - 1)
    def write():
        core = core_ref[0]
        size = acc.shape[1] // (2 * blocks)
        for b in range(blocks):
            here = pl.ds(b * size, size)
            own = pl.ds(pl.multiple_of((2 * b + core) * size, size), size)
            far = pl.ds(pl.multiple_of((2 * b + 1 - core) * size, size), size)
            keep_ref[:, here] = acc[:, own].astype(keep_ref.dtype)
            give_ref[:, here] = acc[:, far].astype(give_ref.dtype)


def run_expert(core, x, weight, gate_matrix, up_matrix, down_matrix, blocks):
    rows, width = x.shape
    hidden = gate_matrix.shape[1]
    tile = 256 if hidden % 256 == 0 else 128
    half = jax.ShapeDtypeStruct((rows, width // 2), jnp.bfloat16)
    return pl.pallas_call(
        functools.partial(expert_kernel, blocks),
        out_shape=(half, half),
        grid_spec=pltpu.PrefetchScalarGridSpec(
            num_scalar_prefetch=1,
            grid=(hidden // tile,),
            in_specs=[
                pl.BlockSpec((rows, width), lambda i, c: (0, 0)),
                pl.BlockSpec((rows, 1), lambda i, c: (0, 0)),
                pl.BlockSpec((width, tile), lambda i, c: (0, i)),
                pl.BlockSpec((width, tile), lambda i, c: (0, i)),
                pl.BlockSpec((tile, width), lambda i, c: (i, 0)),
            ],
            out_specs=[pl.BlockSpec((rows, width // 2), lambda i, c: (0, 0))] * 2,
            scratch_shapes=[pltpu.VMEM((rows, width), jnp.float32)],
        ),
        compiler_params=pltpu.CompilerParams(
            dimension_semantics=("arbitrary",), vmem_limit_bytes=48 * 1024 * 1024
        ),
        cost_estimate=pl.CostEstimate(
            flops=6 * rows * width * hidden,
            bytes_accessed=6 * width * hidden,
            transcendentals=rows * hidden,
        ),
    )(core, x, weight, gate_matrix, up_matrix, down_matrix)


def groups_of(experts):
    steps = list(range(experts))
    return [steps[:1]] + [steps[i : i + 2] for i in range(1, experts - 1, 2)] + [steps[-1:]]


def per_device(tokens, router_gates, routes, gate_proj, up_proj, down_proj):
    experts = lax.axis_size("expert")
    groups = lax.axis_size("ffn")
    rows, width = tokens.shape
    col_width = width // groups
    blocks = groups // 2
    half_rows = rows // 2
    me = lax.axis_index("expert")
    group = lax.axis_index("ffn")
    core = group % 2
    block = group // 2
    core_word = jnp.full((1,), core, jnp.int32)
    gate_matrix, up_matrix, down_matrix = gate_proj[0], up_proj[0], down_proj[0]

    routes_t, gates_t = routes.T, router_gates.T
    names = jnp.arange(experts, dtype=jnp.int32)[:, None]
    dense = sum(
        jnp.where(routes_t[k][None, :] == names, gates_t[k][None, :], 0.0)
        for k in range(routes.shape[1])
    )

    half = lax.dynamic_slice_in_dim(tokens, core * half_rows, half_rows, 0)
    first_steps = list(range(1, experts))[:2]
    fetched, paired = {}, {}
    for step in first_steps:
        fetched[step] = swap(half, "expert", step)
    for step in first_steps:
        paired[step] = swap(fetched[step], "ffn", 1)
    for step in range(3, experts):
        source = after(half, *[paired[s] for s in first_steps])
        fetched[step] = swap(source, "expert", step)
    weights = {0: lax.dynamic_index_in_dim(dense, me, 0, keepdims=False)}
    for step in range(1, experts):
        column = lax.dynamic_index_in_dim(dense, me ^ step, 0, keepdims=False)
        weights[step] = swap(column, "expert", step)

    def chunk_of(steps):
        if steps == [0]:
            return tokens
        parts = []
        for step in steps:
            mine = fetched[step]
            other = paired[step] if step in paired else swap(mine, "ffn", 1)
            parts += [jnp.where(core == 0, mine, other), jnp.where(core == 0, other, mine)]
        return jnp.concatenate(parts, axis=0)

    parts = 2
    size = rows // parts
    returned, previous = [], None
    every = groups_of(experts)
    for number, steps in enumerate(every):
        chunk = chunk_of(steps)
        if number > 1:
            chunk = after(chunk, previous)
        weight = jnp.concatenate([weights[s] for s in steps])[:, None]
        keep, give = run_expert(
            core_word, chunk, weight, gate_matrix, up_matrix, down_matrix, blocks
        )
        got = swap(give, "ffn", 1)
        total = (keep.astype(jnp.float32) + got.astype(jnp.float32)).astype(jnp.bfloat16)
        previous = total
        for at, step in enumerate(steps):
            mine = total[at * rows : (at + 1) * rows]
            pieces = [mine[p * size : (p + 1) * size] for p in range(parts)]
            if step > 0:
                if number < len(every) - 1:
                    moved = swap(mine, "expert", step)
                    pieces = [moved[p * size : (p + 1) * size] for p in range(parts)]
                else:
                    pieces = [swap(p, "expert", step) for p in pieces]
            returned.append(pieces)

    mixed, summed = [], None
    for p in range(parts):
        if p > 0:
            returned[-1][p] = after(returned[-1][p], summed)
        summed = sum(r[p].astype(jnp.float32) for r in returned).astype(jnp.bfloat16)

        def piece(index):
            return lax.dynamic_slice_in_dim(summed, index * col_width, col_width, 1)

        result = piece(block).astype(jnp.float32)
        for step in range(1, blocks):
            moved = swap(piece(block ^ step), "ffn", 2 * step)
            result = result + moved.astype(jnp.float32)
        mixed.append(result.astype(jnp.bfloat16))
    return jnp.concatenate(mixed, axis=0)


def solution(mesh):
    in_specs = (
        P("expert", None),
        P("expert", None),
        P("expert", None),
        P("expert", None, "ffn"),
        P("expert", None, "ffn"),
        P("expert", "ffn", None),
    )
    out_specs = P("expert", "ffn")

    return jax.shard_map(
        per_device, mesh=mesh, in_specs=in_specs, out_specs=out_specs, check_vma=False
    )
```

time: 287 us -> 222 us (0.77)
  blocking collectives: 97.8 us -> 0 us
  Pallas kernels: 0 us -> 72.3 us
  matrix products: 65.9 us -> 0 us
  starting transfers between devices: 3.65 us -> 29.9 us
  between operations: 13.5 us -> 0.21 us
  other arithmetic: 3.72 us -> 14.2 us
  local copies, waits for them, and re-layouts: 1.69 us -> 5.09 us
    ppermute x0 -> x22, waiting for transfers between devices: none -> 100 us  [swap(): return lax.ppermute(value, axis, [(i, i ^ bit) for i in range(size)])]
    all_to_all x1 -> x0, blocking collectives: 97.8 us -> none  [per_device(): lax.all_to_all(outgoing, 'expert', split_axis=0, concat_axis=0, tiled=True)]
    reduce_scatter x1 -> x0, waiting for transfers between devices: 89.4 us -> none  [per_device(): lax.psum_scatter(lax.dot_general(down_matrix, hidden, (((0,), (1,)), ((),...]
    pallas_call x0 -> x3, Pallas kernels: none -> 72.3 us  [run_expert(): pl.pallas_call(functools.partial(expert_kernel, blocks), out_shape=(half,...]
    dot_general x5 -> x0, matrix products: 65.9 us -> none  [the longest x1 21.1 us: per_device(): up_act = jnp.dot(arrived, up_matrix, preferred_element_type=jnp.float32)]
    ppermute x0 -> x22, starting transfers between devices: none -> 29.9 us  [swap(): return lax.ppermute(value, axis, [(i, i ^ bit) for i in range(size)])]
    all_to_all x1 -> x0, waiting for transfers between devices: 10.6 us -> none  [per_device(): lax.all_to_all(summed.reshape(col_width, experts, capacity).astype(jnp.bf...]
    convert_element_type x1 -> x7, other arithmetic: 0.01 us -> 7.85 us  [the longest x3 6.91 us: per_device(): (keep.astype(jnp.float32) + got.astype(jnp.float32)).astype(jnp.bfloat16)]
  transfers between devices with their start and end apart: 2 -> 22, of which waited for: 2 -> 11; matrix products, arithmetic and copies ran while one was open for 0% -> 6% of each run, Pallas kernels for 0% -> 23%
where the time goes in v1:
time: 222 us
  waiting for transfers between devices  100 us (45%)
  Pallas kernels  72.3 us (33%)
  starting transfers between devices  29.9 us (13%)
  other arithmetic  14.2 us (6%)
  local copies, waits for them, and re-layouts  5.09 us (2%)
    ppermute x22, waiting for transfers between devices, swap(): return lax.ppermute(value, axis, [(i, i ^ bit) for i in range(size)])  100 us
    pallas_call x3, Pallas kernels, run_expert(): pl.pallas_call(functools.partial(expert_kernel, blocks), out_shape=(half,...  72.3 us
    ppermute x22, starting transfers between devices, swap(): return lax.ppermute(value, axis, [(i, i ^ bit) for i in range(size)])  29.9 us
    convert_element_type x3, other arithmetic, per_device(): (keep.astype(jnp.float32) + got.astype(jnp.float32)).astype(jnp.bfloat16)  6.91 us
  transfers between devices with their start and end apart: 22, of which 11 were waited for; matrix products, arithmetic and copies ran while one was open for 6% of the time, Pallas kernels for 23%

profile of v1, /device:TPU:0, one launch (start us, length us, event | category | flops | bytes accessed | tf_op | source)
XLA Modules:
  0.0 221.9 jit_solution(7890553724618443136)
XLA Ops:
  0.0 1.3 constant_dynamic-slice_fusion.9
  1.3 3.1 %collective-permute-start.3 = (bf16[128,4096]{1,0:T(8,128)(2,1)S(1)}, bf16[128,4096]{1,0:T(8,128)(2,1)S(1)}, u32[]{:S(2)}, u32[]{:S(2)}) collective-permute-start(bf16[128,4096]{1,0:T(8,128)(2,1)S(1)} %constant_dynamic-slice_fusion.9), channel_id=1, source_target_pairs={{0,16},{8,24},{16,0},{24,8},{1,17},{9,25},{17,1},{25,9},{2,18},{10... | collective-permute-start | bytes 3145736 | tf_op jit(solution)/shard_map/ppermute | solution.py:13
  4.4 1.5 collective-permute-start.1
  5.9 21.7 %collective-permute-done.3 = bf16[128,4096]{1,0:T(8,128)(2,1)S(1)} collective-permute-done((bf16[128,4096]{1,0:T(8,128)(2,1)S(1)}, bf16[128,4096]{1,0:T(8,128)(2,1)S(1)}, u32[]{:S(2)}, u32[]{:S(2)}) %collective-permute-start.3) | collective-permute-done | bytes 1048608 | tf_op jit(solution)/shard_map/ppermute | solution.py:13
  27.5 0.0 collective-permute-start.4
  27.5 1.5 collective-permute-done.1
  29.0 0.0 collective-permute-start.2
  29.0 0.8 fusion.4
  29.8 0.8 fusion.3
  30.5 0.9 collective-permute-start.6
  31.4 1.5 collective-permute-start.5
  32.9 1.3 collective-permute-done.6
  34.2 0.8 collective-permute-done.5
  35.0 0.1 copy.8.w_ref
  35.1 0.0 collective-permute-done.4
  35.1 0.0 collective-permute-done.2
  35.2 2.2 %collective-permute-start.10 = (bf16[128,4096]{1,0:T(8,128)(2,1)}, bf16[128,4096]{1,0:T(8,128)(2,1)}, u32[]{:S(2)}, u32[]{:S(2)}) collective-permute-start(bf16[128,4096]{1,0:T(8,128)(2,1)} %copy-done.1), channel_id=1, source_target_pairs={{0,24},{8,16},{16,8},{24,0},{1,25},{9,17},{17,9},{25,1},{2,26},{10... | collective-permute-start | bytes 3145736 | tf_op jit(solution)/shard_map/ppermute | solution.py:13
  37.4 0.1 broadcast_select_fusion.3
  37.5 1.4 broadcast_select_fusion.5
  38.9 2.3 %pad_maximum_fusion.x_ref = bf16[512,4096]{1,0:T(8,128)(2,1)} fusion(bf16[128,4096]{1,0:T(8,128)(2,1)S(1)} %get-tuple-element.28, bf16[128,4096]{1,0:T(8,128)(2,1)S(1)} %get-tuple-element.27, bf16[128,4096]{1,0:T(8,128)(2,1)S(1)} %get-tuple-element.26, bf16[128,4096]{1,0:T(8,128)(2,1)S(1)} %get-tuple-element.25), kind=kLoop, calls=%fused_computation | loop fusion | flops 16777216 | bytes 8388608 | tf_op jit(solution)/shard_map/concatenate | solution.py:127
  41.2 19.0 %collective-permute-done.10 = bf16[128,4096]{1,0:T(8,128)(2,1)} collective-permute-done((bf16[128,4096]{1,0:T(8,128)(2,1)}, bf16[128,4096]{1,0:T(8,128)(2,1)}, u32[]{:S(2)}, u32[]{:S(2)}) %collective-permute-start.10) | collective-permute-done | bytes 1048608 | tf_op jit(solution)/shard_map/ppermute | solution.py:13
  60.1 0.0 collective-permute-start.11
  60.2 31.4 %shard_map.65 = (bf16[512,2048]{1,0:T(8,128)(2,1)S(1)}, bf16[512,2048]{1,0:T(8,128)(2,1)}) custom-call(s32[1]{0:T(128)} %bitcast.core_ref, bf16[512,4096]{1,0:T(8,128)(2,1)} %pad_maximum_fusion.x_ref, f32[512,1]{1,0:T(8,128)S(1)} %copy.8.w_ref, bf16[4096,1792]{1,0:T(8,128)(2,1)} %bitcast.17, bf16[4096,1792]{1,0:T(8,128)(2,1)} %bitcast.20, ...), custom_call_target="tpu_custom_call" | custom-call | flops 22548578304 | bytes 44040192 | tf_op jit(solution)/shard_map/pallas_call | solution.py:51
  91.6 0.5 collective-permute-start.7
  92.1 2.6 %collective-permute-start.12 = (f32[256]{0:T(256)S(1)}, f32[256]{0:T(256)S(1)}, u32[]{:S(2)}, u32[]{:S(2)}) collective-permute-start(f32[256]{0:T(256)S(1)} %bitcast.34), channel_id=1, source_target_pairs={{0,24},{8,16},{16,8},{24,0},{1,25},{9,17},{17,9},{25,1},{2,26},{10... | collective-permute-start | bytes 3080 | tf_op jit(solution)/shard_map/ppermute | solution.py:13
  94.7 0.1 copy.7.w_ref
  94.8 1.7 collective-permute-done.12
  96.5 0.1 copy.9.w_ref
  96.7 0.0 collective-permute-done.11
  96.7 1.7 broadcast_select_fusion.1
  98.4 0.2 pad_maximum_fusion.1.x_ref
  98.6 3.7 %add_convert_fusion = bf16[512,2048]{1,0:T(8,128)(2,1)} fusion(bf16[512,2048]{1,0:T(8,128)(2,1)} %collective-permute-done.7, bf16[512,2048]{1,0:T(8,128)(2,1)S(1)} %get-tuple-element.16), kind=kLoop, calls=%fused_computation.1 | loop fusion | flops 4194304 | bytes 6291456 | tf_op jit(solution)/shard_map/convert_element_type | solution.py:142
  102.3 20.9 %shard_map.66 = (bf16[256,2048]{1,0:T(8,128)(2,1)S(1)}, bf16[256,2048]{1,0:T(8,128)(2,1)}) custom-call(s32[1]{0:T(128)} %bitcast.core_ref, bf16[256,4096]{1,0:T(8,128)(2,1)S(1)} %pad_maximum_fusion.1.x_ref, f32[256,1]{1,0:T(8,128)S(1)} %copy.9.w_ref, bf16[4096,1792]{1,0:T(8,128)(2,1)} %bitcast.18, bf16[4096,1792]{1,0:T(8,128)(2,1)} %bitcast.21, ...), custom_call_target="tpu_custom_call" | custom-call | flops 11274289152 | bytes 44040192 | tf_op jit(solution)/shard_map/pallas_call | solution.py:51
  123.2 0.0 collective-permute-start.13
  123.2 20.0 %shard_map.64 = (bf16[256,2048]{1,0:T(8,128)(2,1)S(1)}, bf16[256,2048]{1,0:T(8,128)(2,1)S(1)}) custom-call(s32[1]{0:T(128)} %bitcast.core_ref, bf16[256,4096]{1,0:T(8,128)(2,1)S(1)} %copy-done, f32[256,1]{1,0:T(8,128)S(1)} %copy.7.w_ref, bf16[4096,1792]{1,0:T(8,128)(2,1)} %bitcast.19, bf16[4096,1792]{1,0:T(8,128)(2,1)} %bitcast.22, bf16[1792,4096]{1,0:T(8,128)(2,1)} %bitcast.25), custom_call_target="tpu_custom_call" | custom-call | flops 11274289152 | bytes 44040192 | tf_op jit(solution)/shard_map/pallas_call | solution.py:51
  143.1 0.6 collective-permute-start
  143.7 1.7 fusion.1
  145.4 1.7 collective-permute-start.8
  147.1 1.5 collective-permute-start.9
  148.6 1.6 add_convert_fusion.1
  150.2 0.1 fusion.2
  150.3 0.4 collective-permute-start.14
  150.7 2.6 %collective-permute-start.18 = (bf16[128,2048]{1,0:T(8,128)(2,1)S(1)}, bf16[128,2048]{1,0:T(8,128)(2,1)S(1)}, u32[]{:S(2)}, u32[]{:S(2)}) collective-permute-start(bf16[128,2048]{1,0:T(8,128)(2,1)S(1)} %get-tuple-element.32), channel_id=1, source_target_pairs={{0,24},{8,16},{16,8},{24,0},{1,25},{9,17},{17,9},{25,1},{2,26},{10... | collective-permute-start | bytes 1572872 | tf_op jit(solution)/shard_map/ppermute | solution.py:13
  153.3 0.0 collective-permute-done
  153.3 1.6 add_convert_fusion.2
  154.9 16.5 %collective-permute-done.8 = bf16[256,2048]{1,0:T(8,128)(2,1)S(1)} collective-permute-done((bf16[256,2048]{1,0:T(8,128)(2,1)S(1)}, bf16[256,2048]{1,0:T(8,128)(2,1)S(1)}, u32[]{:S(2)}, u32[]{:S(2)}) %collective-permute-start.8) | collective-permute-done | bytes 1048608 | tf_op jit(solution)/shard_map/ppermute | solution.py:13
  171.5 22.9 %collective-permute-done.9 = bf16[256,2048]{1,0:T(8,128)(2,1)S(1)} collective-permute-done((bf16[256,2048]{1,0:T(8,128)(2,1)S(1)}, bf16[256,2048]{1,0:T(8,128)(2,1)S(1)}, u32[]{:S(2)}, u32[]{:S(2)}) %collective-permute-start.9) | collective-permute-done | bytes 1048608 | tf_op jit(solution)/shard_map/ppermute | solution.py:13
  194.4 0.0 collective-permute-done.14
  194.4 0.4 add_convert_fusion.4
  194.8 0.0 collective-permute-done.18
  194.8 0.4 add_convert_fusion.3
  195.2 1.6 collective-permute-start.19
  196.9 2.5 %collective-permute-start.21 = (bf16[128,512]{1,0:T(8,128)(2,1)S(1)}, bf16[128,512]{1,0:T(8,128)(2,1)S(1)}, u32[]{:S(2)}, u32[]{:S(2)}) collective-permute-start(bf16[128,512]{1,0:T(8,128)(2,1)S(1)} %get-tuple-element.37), channel_id=1, source_target_pairs={{0,6},{1,7},{2,4},{3,5},{4,2},{5,3},{6,0},{7,1},{8,14},{9,15},{10,... | collective-permute-start | bytes 393224 | tf_op jit(solution)/shard_map/ppermute | solution.py:13
  199.4 0.1 collective-permute-start.20
  199.5 1.9 collective-permute-start.15
  201.4 2.5 %collective-permute-start.17 = (bf16[128,512]{1,0:T(8,128)(2,1)S(1)}, bf16[128,512]{1,0:T(8,128)(2,1)S(1)}, u32[]{:S(2)}, u32[]{:S(2)}) collective-permute-start(bf16[128,512]{1,0:T(8,128)(2,1)S(1)} %get-tuple-element.34), channel_id=1, source_target_pairs={{0,6},{1,7},{2,4},{3,5},{4,2},{5,3},{6,0},{7,1},{8,14},{9,15},{10,... | collective-permute-start | bytes 393224 | tf_op jit(solution)/shard_map/ppermute | solution.py:13
  203.9 2.3 %collective-permute-start.16 = (bf16[128,512]{1,0:T(8,128)(2,1)S(1)}, bf16[128,512]{1,0:T(8,128)(2,1)S(1)}, u32[]{:S(2)}, u32[]{:S(2)}) collective-permute-start(bf16[128,512]{1,0:T(8,128)(2,1)S(1)} %get-tuple-element.35), channel_id=1, source_target_pairs={{0,4},{1,5},{2,6},{3,7},{4,0},{5,1},{6,2},{7,3},{8,12},{9,13},{10,... | collective-permute-start | bytes 393224 | tf_op jit(solution)/shard_map/ppermute | solution.py:13
  206.2 0.4 collective-permute-done.21
  206.5 10.3 %collective-permute-done.20 = bf16[128,512]{1,0:T(8,128)(2,1)S(1)} collective-permute-done((bf16[128,512]{1,0:T(8,128)(2,1)S(1)}, bf16[128,512]{1,0:T(8,128)(2,1)S(1)}, u32[]{:S(2)}, u32[]{:S(2)}) %collective-permute-start.20) | collective-permute-done | bytes 131104 | tf_op jit(solution)/shard_map/ppermute | solution.py:13
  216.9 0.1 add_convert_fusion.5
  216.9 0.0 collective-permute-done.15
  217.0 4.1 %collective-permute-done.16 = bf16[128,512]{1,0:T(8,128)(2,1)S(1)} collective-permute-done((bf16[128,512]{1,0:T(8,128)(2,1)S(1)}, bf16[128,512]{1,0:T(8,128)(2,1)S(1)}, u32[]{:S(2)}, u32[]{:S(2)}) %collective-permute-start.16) | collective-permute-done | bytes 131104 | tf_op jit(solution)/shard_map/ppermute | solution.py:13
  221.1 0.1 add_convert_fusion.6
  221.2 0.7 pad_maximum_fusion.2
  (13 shorter events, 0.1 us)
Async XLA Ops:
  1.3 27.7 %copy-start.1 = (bf16[128,4096]{1,0:T(8,128)(2,1)}, bf16[128,4096]{1,0:T(8,128)(2,1)S(1)}, u32[]{:S(2)}) copy-start(bf16[128,4096]{1,0:T(8,128)(2,1)S(1)} %constant_dynamic-slice_fusion.9) | copy-start | bytes 3145732
  1.3 26.2 %collective-permute-start.3 = (bf16[128,4096]{1,0:T(8,128)(2,1)S(1)}, bf16[128,4096]{1,0:T(8,128)(2,1)S(1)}, u32[]{:S(2)}, u32[]{:S(2)}) collective-permute-start(bf16[128,4096]{1,0:T(8,128)(2,1)S(1)} %constant_dynamic-slice_fusion.9), channel_id=1, source_target_pairs={{0,16},{8,24},{16,0},{24,8},{1,17},{9,25},{17,1},{25,9},{2,18},{10... | collective-permute-start | bytes 3145736 | tf_op jit(solution)/shard_map/ppermute | solution.py:13
  4.4 24.6 %collective-permute-start.1 = (bf16[128,4096]{1,0:T(8,128)(2,1)S(1)}, bf16[128,4096]{1,0:T(8,128)(2,1)S(1)}, u32[]{:S(2)}, u32[]{:S(2)}) collective-permute-start(bf16[128,4096]{1,0:T(8,128)(2,1)S(1)} %constant_dynamic-slice_fusion.9), channel_id=1, source_target_pairs={{0,8},{8,0},{16,24},{24,16},{1,9},{9,1},{17,25},{25,17},{2,10},{10... | collective-permute-start | bytes 3145736 | tf_op jit(solution)/shard_map/ppermute | solution.py:13
  27.5 7.6 %collective-permute-start.4 = (bf16[128,4096]{1,0:T(8,128)(2,1)S(1)}, bf16[128,4096]{1,0:T(8,128)(2,1)S(1)}, u32[]{:S(2)}, u32[]{:S(2)}) collective-permute-start(bf16[128,4096]{1,0:T(8,128)(2,1)S(1)} %collective-permute-done.3), channel_id=1, source_target_pairs={{0,1},{1,0},{2,3},{3,2},{4,5},{5,4},{6,7},{7,6},{8,9},{9,8},{10,11... | collective-permute-start | bytes 3145736 | tf_op jit(solution)/shard_map/ppermute | solution.py:13
  29.0 6.2 %collective-permute-start.2 = (bf16[128,4096]{1,0:T(8,128)(2,1)S(1)}, bf16[128,4096]{1,0:T(8,128)(2,1)}, u32[]{:S(2)}, u32[]{:S(2)}) collective-permute-start(bf16[128,4096]{1,0:T(8,128)(2,1)S(1)} %collective-permute-done.1), channel_id=1, source_target_pairs={{0,1},{1,0},{2,3},{3,2},{4,5},{5,4},{6,7},{7,6},{8,9},{9,8},{10,11... | collective-permute-start | bytes 3145736 | tf_op jit(solution)/shard_map/ppermute | solution.py:13
  30.5 3.6 %collective-permute-start.6 = (f32[256]{0:T(256)S(1)}, f32[256]{0:T(256)S(1)}, u32[]{:S(2)}, u32[]{:S(2)}) collective-permute-start(f32[256]{0:T(256)S(1)} %bitcast.36), channel_id=1, source_target_pairs={{0,16},{8,24},{16,0},{24,8},{1,17},{9,25},{17,1},{25,9},{2,18},{10... | collective-permute-start | bytes 3080 | tf_op jit(solution)/shard_map/ppermute | solution.py:13
  31.4 3.6 %collective-permute-start.5 = (f32[256]{0:T(256)S(1)}, f32[256]{0:T(256)S(1)}, u32[]{:S(2)}, u32[]{:S(2)}) collective-permute-start(f32[256]{0:T(256)S(1)} %bitcast.35), channel_id=1, source_target_pairs={{0,8},{8,0},{16,24},{24,16},{1,9},{9,1},{17,25},{25,17},{2,10},{10... | collective-permute-start | bytes 3080 | tf_op jit(solution)/shard_map/ppermute | solution.py:13
  35.2 25.0 %collective-permute-start.10 = (bf16[128,4096]{1,0:T(8,128)(2,1)}, bf16[128,4096]{1,0:T(8,128)(2,1)}, u32[]{:S(2)}, u32[]{:S(2)}) collective-permute-start(bf16[128,4096]{1,0:T(8,128)(2,1)} %copy-done.1), channel_id=1, source_target_pairs={{0,24},{8,16},{16,8},{24,0},{1,25},{9,17},{17,9},{25,1},{2,26},{10... | collective-permute-start | bytes 3145736 | tf_op jit(solution)/shard_map/ppermute | solution.py:13
  60.1 36.5 %collective-permute-start.11 = (bf16[128,4096]{1,0:T(8,128)(2,1)}, bf16[128,4096]{1,0:T(8,128)(2,1)}, u32[]{:S(2)}, u32[]{:S(2)}) collective-permute-start(bf16[128,4096]{1,0:T(8,128)(2,1)} %collective-permute-done.10), channel_id=1, source_target_pairs={{0,1},{1,0},{2,3},{3,2},{4,5},{5,4},{6,7},{7,6},{8,9},{9,8},{10,11... | collective-permute-start | bytes 3145736 | tf_op jit(solution)/shard_map/ppermute | solution.py:13
  91.6 7.0 %collective-permute-start.7 = (bf16[512,2048]{1,0:T(8,128)(2,1)}, bf16[512,2048]{1,0:T(8,128)(2,1)}, u32[]{:S(2)}, u32[]{:S(2)}) collective-permute-start(bf16[512,2048]{1,0:T(8,128)(2,1)} %get-tuple-element.17), channel_id=1, source_target_pairs={{0,1},{1,0},{2,3},{3,2},{4,5},{5,4},{6,7},{7,6},{8,9},{9,8},{10,11... | collective-permute-start | bytes 6291464 | tf_op jit(solution)/shard_map/ppermute | solution.py:13
  92.1 4.5 %collective-permute-start.12 = (f32[256]{0:T(256)S(1)}, f32[256]{0:T(256)S(1)}, u32[]{:S(2)}, u32[]{:S(2)}) collective-permute-start(f32[256]{0:T(256)S(1)} %bitcast.34), channel_id=1, source_target_pairs={{0,24},{8,16},{16,8},{24,0},{1,25},{9,17},{17,9},{25,1},{2,26},{10... | collective-permute-start | bytes 3080 | tf_op jit(solution)/shard_map/ppermute | solution.py:13
  102.3 20.9 %copy-start = (bf16[256,4096]{1,0:T(8,128)(2,1)S(1)}, bf16[256,4096]{1,0:T(8,128)(2,1)}, u32[]{:S(2)}) copy-start(bf16[256,4096]{1,0:T(8,128)(2,1)} %x_ref.1) | copy-start | bytes 6291460
  123.2 25.4 %collective-permute-start.13 = (bf16[256,2048]{1,0:T(8,128)(2,1)}, bf16[256,2048]{1,0:T(8,128)(2,1)}, u32[]{:S(2)}, u32[]{:S(2)}) collective-permute-start(bf16[256,2048]{1,0:T(8,128)(2,1)} %get-tuple-element.21), channel_id=1, source_target_pairs={{0,1},{1,0},{2,3},{3,2},{4,5},{5,4},{6,7},{7,6},{8,9},{9,8},{10,11... | collective-permute-start | bytes 3145736 | tf_op jit(solution)/shard_map/ppermute | solution.py:13
  143.1 10.2 %collective-permute-start = (bf16[256,2048]{1,0:T(8,128)(2,1)S(1)}, bf16[256,2048]{1,0:T(8,128)(2,1)}, u32[]{:S(2)}, u32[]{:S(2)}) collective-permute-start(bf16[256,2048]{1,0:T(8,128)(2,1)S(1)} %get-tuple-element.15), channel_id=1, source_target_pairs={{0,1},{1,0},{2,3},{3,2},{4,5},{5,4},{6,7},{7,6},{8,9},{9,8},{10,11... | collective-permute-start | bytes 3145736 | tf_op jit(solution)/shard_map/ppermute | solution.py:13
  145.4 26.1 %collective-permute-start.8 = (bf16[256,2048]{1,0:T(8,128)(2,1)S(1)}, bf16[256,2048]{1,0:T(8,128)(2,1)S(1)}, u32[]{:S(2)}, u32[]{:S(2)}) collective-permute-start(bf16[256,2048]{1,0:T(8,128)(2,1)S(1)} %get-tuple-element.23), channel_id=1, source_target_pairs={{0,8},{8,0},{16,24},{24,16},{1,9},{9,1},{17,25},{25,17},{2,10},{10... | collective-permute-start | bytes 3145736 | tf_op jit(solution)/shard_map/ppermute | solution.py:13
  147.1 47.3 %collective-permute-start.9 = (bf16[256,2048]{1,0:T(8,128)(2,1)S(1)}, bf16[256,2048]{1,0:T(8,128)(2,1)S(1)}, u32[]{:S(2)}, u32[]{:S(2)}) collective-permute-start(bf16[256,2048]{1,0:T(8,128)(2,1)S(1)} %get-tuple-element.24), channel_id=1, source_target_pairs={{0,16},{8,24},{16,0},{24,8},{1,17},{9,25},{17,1},{25,9},{2,18},{10... | collective-permute-start | bytes 3145736 | tf_op jit(solution)/shard_map/ppermute | solution.py:13
  150.3 44.1 %collective-permute-start.14 = (bf16[128,2048]{1,0:T(8,128)(2,1)S(1)}, bf16[128,2048]{1,0:T(8,128)(2,1)S(1)}, u32[]{:S(2)}, u32[]{:S(2)}) collective-permute-start(bf16[128,2048]{1,0:T(8,128)(2,1)S(1)} %get-tuple-element.31), channel_id=1, source_target_pairs={{0,24},{8,16},{16,8},{24,0},{1,25},{9,17},{17,9},{25,1},{2,26},{10... | collective-permute-start | bytes 1572872 | tf_op jit(solution)/shard_map/ppermute | solution.py:13
  150.7 44.1 %collective-permute-start.18 = (bf16[128,2048]{1,0:T(8,128)(2,1)S(1)}, bf16[128,2048]{1,0:T(8,128)(2,1)S(1)}, u32[]{:S(2)}, u32[]{:S(2)}) collective-permute-start(bf16[128,2048]{1,0:T(8,128)(2,1)S(1)} %get-tuple-element.32), channel_id=1, source_target_pairs={{0,24},{8,16},{16,8},{24,0},{1,25},{9,17},{17,9},{25,1},{2,26},{10... | collective-permute-start | bytes 1572872 | tf_op jit(solution)/shard_map/ppermute | solution.py:13
  195.2 8.6 %collective-permute-start.19 = (bf16[128,512]{1,0:T(8,128)(2,1)S(1)}, bf16[128,512]{1,0:T(8,128)(2,1)S(1)}, u32[]{:S(2)}, u32[]{:S(2)}) collective-permute-start(bf16[128,512]{1,0:T(8,128)(2,1)S(1)} %get-tuple-element.36), channel_id=1, source_target_pairs={{0,2},{1,3},{2,0},{3,1},{4,6},{5,7},{6,4},{7,5},{8,10},{9,11},{10,... | collective-permute-start | bytes 393224 | tf_op jit(solution)/shard_map/ppermute | solution.py:13
  196.9 9.6 %collective-permute-start.21 = (bf16[128,512]{1,0:T(8,128)(2,1)S(1)}, bf16[128,512]{1,0:T(8,128)(2,1)S(1)}, u32[]{:S(2)}, u32[]{:S(2)}) collective-permute-start(bf16[128,512]{1,0:T(8,128)(2,1)S(1)} %get-tuple-element.37), channel_id=1, source_target_pairs={{0,6},{1,7},{2,4},{3,5},{4,2},{5,3},{6,0},{7,1},{8,14},{9,15},{10,... | collective-permute-start | bytes 393224 | tf_op jit(solution)/shard_map/ppermute | solution.py:13
  199.4 17.5 %collective-permute-start.20 = (bf16[128,512]{1,0:T(8,128)(2,1)S(1)}, bf16[128,512]{1,0:T(8,128)(2,1)S(1)}, u32[]{:S(2)}, u32[]{:S(2)}) collective-permute-start(bf16[128,512]{1,0:T(8,128)(2,1)S(1)} %get-tuple-element.38), channel_id=1, source_target_pairs={{0,4},{1,5},{2,6},{3,7},{4,0},{5,1},{6,2},{7,3},{8,12},{9,13},{10,... | collective-permute-start | bytes 393224 | tf_op jit(solution)/shard_map/ppermute | solution.py:13
  199.5 17.4 %collective-permute-start.15 = (bf16[128,512]{1,0:T(8,128)(2,1)S(1)}, bf16[128,512]{1,0:T(8,128)(2,1)S(1)}, u32[]{:S(2)}, u32[]{:S(2)}) collective-permute-start(bf16[128,512]{1,0:T(8,128)(2,1)S(1)} %get-tuple-element.33), channel_id=1, source_target_pairs={{0,2},{1,3},{2,0},{3,1},{4,6},{5,7},{6,4},{7,5},{8,10},{9,11},{10,... | collective-permute-start | bytes 393224 | tf_op jit(solution)/shard_map/ppermute | solution.py:13
  201.4 15.6 %collective-permute-start.17 = (bf16[128,512]{1,0:T(8,128)(2,1)S(1)}, bf16[128,512]{1,0:T(8,128)(2,1)S(1)}, u32[]{:S(2)}, u32[]{:S(2)}) collective-permute-start(bf16[128,512]{1,0:T(8,128)(2,1)S(1)} %get-tuple-element.34), channel_id=1, source_target_pairs={{0,6},{1,7},{2,4},{3,5},{4,2},{5,3},{6,0},{7,1},{8,14},{9,15},{10,... | collective-permute-start | bytes 393224 | tf_op jit(solution)/shard_map/ppermute | solution.py:13
  203.9 17.2 %collective-permute-start.16 = (bf16[128,512]{1,0:T(8,128)(2,1)S(1)}, bf16[128,512]{1,0:T(8,128)(2,1)S(1)}, u32[]{:S(2)}, u32[]{:S(2)}) collective-permute-start(bf16[128,512]{1,0:T(8,128)(2,1)S(1)} %get-tuple-element.35), channel_id=1, source_target_pairs={{0,4},{1,5},{2,6},{3,7},{4,0},{5,1},{6,2},{7,3},{8,12},{9,13},{10,... | collective-permute-start | bytes 393224 | tf_op jit(solution)/shard_map/ppermute | solution.py:13
